TPU v7x, 32 devices: a whole 2x2x4 slice. The times are simulated.
32 devices in a mesh: ctx: 4 (over x, core), vocab: 8 (over z, y).
Axes of the slice: x: 2, y: 2, z: 4, core: 2. Of those that a mesh axis runs over, the one named last changes fastest.
Arguments:
- hidden: bfloat16 [256, 2, 7168], P('ctx', None, 'vocab'), may hold values from -30 to 30
- head: bfloat16 [7168, 16384], P('ctx', 'vocab'), may hold values from -0.15 to 0.15
- targets: int32 [256, 2], P('ctx'), may hold values from 0 to 16383
- loss_weight: float32 [256, 2], P('ctx'), may hold values from 16 to 256
Outputs:
- token_loss: float32 [256, 2], P('ctx')
- grad_hidden: bfloat16 [256, 2, 7168], P('ctx', None, 'vocab')
All inputs are finite; a program needn't handle non-finite values.
Results may differ from a plain program's by a relative error of at most 0.0046.
Values may be sent and summed in bfloat16 or wider, within the bound.
No kernel may reach another device: no remote copies, remote signals or barrier semaphores. Data moves between devices by JAX's collectives and lax.ppermute only.
A program may use at most 64 MiB of HBM per device.

v0:
```python
import jax
import jax.numpy as jnp
from jax import lax
from jax.sharding import PartitionSpec as P


def body(hidden, head, targets, loss_weight):
    group_rows = hidden.shape[0]
    depth_count = hidden.shape[1]
    flat_count = group_rows * depth_count
    vocab_index = lax.axis_index("vocab")
    vocab_local = head.shape[1]
    flat_hidden = hidden.reshape(flat_count, hidden.shape[2])
    flat_targets = targets.reshape(flat_count)
    flat_weights = loss_weight.reshape(flat_count)
    whole_width = lax.all_gather(flat_hidden, "vocab", axis=1, tiled=True)
    width_slab = lax.all_to_all(whole_width, "ctx", split_axis=1, concat_axis=0, tiled=True)
    logits = lax.psum_scatter(
        jnp.dot(width_slab, head, preferred_element_type=jnp.float32),
        "ctx",
        scatter_dimension=0,
        tiled=True,
    )
    columns = vocab_index * vocab_local + lax.broadcasted_iota(jnp.int32, logits.shape, 1)
    target_hit = columns == flat_targets[:, None]
    local_max = jnp.max(logits, axis=1)
    local_target = jnp.sum(jnp.where(target_hit, logits, 0.0), axis=1)
    row_max = lax.pmax(local_max, "vocab")
    local_sum = jnp.sum(jnp.exp(logits - row_max[:, None]), axis=1)
    sum_exp, target_logit = lax.psum((local_sum, local_target), "vocab")
    flat_loss = jnp.log(sum_exp) + row_max - target_logit
    token_loss = flat_loss.reshape(group_rows, depth_count)
    probabilities = jnp.exp(logits - row_max[:, None]) / sum_exp[:, None]
    dlogits = (flat_weights[:, None] * (probabilities - target_hit.astype(jnp.float32))).astype(
        jnp.bfloat16
    )
    grad_slab = lax.dot_general(
        lax.all_gather(dlogits, "ctx", axis=0, tiled=True),
        head,
        (((1,), (1,)), ((), ())),
        preferred_element_type=jnp.float32,
    )
    returned = lax.all_to_all(grad_slab, "ctx", split_axis=0, concat_axis=1, tiled=True)
    grad_width = lax.psum_scatter(returned, "vocab", scatter_dimension=1, tiled=True)
    grad_out = grad_width.astype(jnp.bfloat16).reshape(group_rows, depth_count, grad_width.shape[1])
    return (token_loss, grad_out)


def solution(mesh):
    return jax.shard_map(
        body,
        mesh=mesh,
        in_specs=(P("ctx", None, "vocab"), P("ctx", "vocab"), P("ctx", None), P("ctx", None)),
        out_specs=(P("ctx", None), P("ctx", None, "vocab")),
        check_vma=False,
    )
```

profile of v0, /device:TPU:0, one launch (start us, length us, event | category | flops | bytes accessed | tf_op | source)
XLA Modules:
  0.0 360.6 jit_solution(2139079968962147869)
XLA Ops:
  7.2 1.7 reshape.23
  9.0 51.1 %all-gather.3.cloned.1.call-done = bf16[128,7168]{1,0:T(8,128)(2,1)} async-done(((bf16[128,896]{1,0:T(8,128)(2,1)}), bf16[128,7168]{1,0:T(8,128)(2,1)}) %all-gather.3.cloned.1.call-update) | async-done | bytes 1835024 | tf_op jit(solution)/shard_map/all_gather | solution.py:16
  60.1 3.3 copy.21
  63.4 26.1 %all_to_all.38 = bf16[128,4,1792]{0,2,1:T(8,128)(2,1)} all-to-all(bf16[128,4,1792]{0,2,1:T(8,128)(2,1)S(1)} %bitcast.12), channel_id=1, replica_groups=mesh['ctx'=4,'vocab'=8] {'ctx'}, dimensions={1} | all-to-all | bytes 3670016 | tf_op jit(solution)/shard_map/all_to_all | solution.py:17
  89.4 2.8 copy.22
  92.2 8.6 %fusion.5 = f32[512,2048]{1,0:T(8,128)} fusion(bf16[512,1792]{1,0:T(8,128)(2,1)S(1)} %bitcast.15, bf16[1792,2048]{1,0:T(8,128)(2,1)} %param.5), kind=kOutput, calls=%fused_computation.10 | convolution fusion | flops 3758096384 | bytes 13369344 | tf_op jit(solution)/shard_map/dot_general | solution.py:19
  100.9 0.6 copy-done
  101.5 0.1 eq.10
  101.8 0.1 mul.14
  101.9 41.5 %reduce-scatter.3.cloned.1.call-done = f32[128,2048]{1,0:T(8,128)} async-done(((f32[512,2048]{1,0:T(8,128)}), f32[128,2048]{1,0:T(8,128)}) %reduce-scatter.3.cloned.1.call-update) | async-done | bytes 1048592 | tf_op jit(solution)/shard_map/reduce_scatter | solution.py:18
  143.5 1.4 reduce_max.9
  144.8 21.4 %pmax.7 = f32[128]{0:T(128)S(1)} all-reduce(f32[128]{0:T(128)S(1)} %reduce_max.9), channel_id=1, replica_groups=mesh['ctx'=4,'vocab'=8] {'vocab'}, use_global_device_ids=true, to_apply=%region_2.3 | all-reduce | flops 128 | bytes 1024 | tf_op jit(solution)/shard_map/pmax | solution.py:28
  166.2 1.6 fusion.4
  167.8 17.1 %all-reduce = (f32[128]{0:T(128)S(1)}, f32[128]{0:T(128)S(1)}) all-reduce(f32[128]{0:T(128)S(1)} %get-tuple-element.11, f32[128]{0:T(128)S(1)} %get-tuple-element.10), channel_id=1, replica_groups=mesh['ctx'=4,'vocab'=8] {'vocab'}, use_global_device_ids=true, to_apply=%region_6.7 | all-reduce | flops 256 | bytes 2048 | tf_op jit(solution)/shard_map/psum | solution.py:30
  184.9 2.4 fusion.3
  187.4 20.4 %all-gather.5.cloned.1.call-done = bf16[512,2048]{1,0:T(8,128)(2,1)} async-done(((bf16[128,2048]{1,0:T(8,128)(2,1)}), bf16[512,2048]{1,0:T(8,128)(2,1)}) %all-gather.5.cloned.1.call-update) | async-done | bytes 2097168 | tf_op jit(solution)/shard_map/all_gather | solution.py:38
  207.8 9.5 %fusion.6 = f32[512,1792]{1,0:T(8,128)} fusion(bf16[512,2048]{1,0:T(8,128)(2,1)} %all-gather.5.cloned.1.call-done, bf16[1792,2048]{1,0:T(8,128)(2,1)} %param.5), kind=kOutput, calls=%fused_computation.11 | convolution fusion | flops 3758096384 | bytes 13107200 | tf_op jit(solution)/shard_map/dot_general | solution.py:37
  217.4 5.1 %copy.25 = f32[4,128,1792]{1,2,0:T(8,128)} copy(f32[4,128,1792]{2,1,0:T(8,128)} %bitcast.14) | data formatting | bytes 7340032 | tf_op jit(solution)/shard_map/all_to_all | solution.py:43
  222.5 48.1 %all_to_all.39 = f32[4,128,1792]{1,2,0:T(8,128)} all-to-all(f32[4,128,1792]{1,2,0:T(8,128)} %copy.25), channel_id=1, replica_groups=mesh['ctx'=4,'vocab'=8] {'ctx'}, dimensions={0} | all-to-all | bytes 7340032 | tf_op jit(solution)/shard_map/all_to_all | solution.py:43
  270.8 0.6 copy.27
  271.4 80.7 %reduce-scatter.5.cloned.1.call-done = f32[128,896]{0,1:T(8,128)} async-done(((f32[128,7168]{0,1:T(8,128)}), f32[128,896]{0,1:T(8,128)}) %reduce-scatter.5.cloned.1.call-update) | async-done | bytes 458768 | tf_op jit(solution)/shard_map/reduce_scatter | solution.py:44
  352.1 1.0 convert_element_type.11
  353.1 0.2 copy.26
  353.3 0.8 reshape.25
  (16 shorter events, 0.6 us)
Async XLA Ops:
  7.2 52.9 %all-gather.3.cloned.1.call-start = ((), (), s32[]{:S(2)}) async-start(), calls=%async_computation.4 | async-start | bytes 2064384 | tf_op jit(solution)/shard_map/all_gather | solution.py:16
  8.9 134.5 %reduce-scatter.3.cloned.1.call-start = ((), (), s32[]{:S(2)}) async-start(), calls=%async_computation.5 | async-start | bytes 5242880 | tf_op jit(solution)/shard_map/reduce_scatter | solution.py:18
  100.8 0.7 copy-start
  100.8 0.9 copy-start.1
  100.8 107.0 %all-gather.5.cloned.1.call-start = ((), (), s32[]{:S(2)}) async-start(), calls=%async_computation.6 | async-start | bytes 2621440 | tf_op jit(solution)/shard_map/all_gather | solution.py:38
  187.4 164.7 %reduce-scatter.5.cloned.1.call-start = ((), (), s32[]{:S(2)}) async-start(), calls=%async_computation.7 | async-start | bytes 4128768 | tf_op jit(solution)/shard_map/reduce_scatter | solution.py:44
Sparse Core Ops, SparseCore 0:
  10.8 49.2 all-gather.2
  100.9 42.4 reduce-scatter.2
  187.5 20.3 all-gather.4
  270.7 81.2 reduce-scatter.4
where the time goes:
time: 361 us
  waiting for transfers between devices  194 us (54%)
  blocking collectives  113 us (31%)
  matrix products  18.1 us (5%)
  local copies, waits for them, and re-layouts  15.7 us (4%)
  between operations  13.8 us (4%)
  other arithmetic  6.43 us (2%)
    reduce_scatter x1, waiting for transfers between devices, body(): lax.psum_scatter(returned, 'vocab', scatter_dimension=1, tiled=True)  80.7 us
    all_gather x1, waiting for transfers between devices, body(): whole_width = lax.all_gather(flat_hidden, 'vocab', axis=1, tiled=True)  51.1 us
    all_to_all x1, blocking collectives, body(): lax.all_to_all(grad_slab, 'ctx', split_axis=0, concat_axis=1, tiled=True)  48.1 us
    reduce_scatter x1, waiting for transfers between devices, body(): lax.psum_scatter(jnp.dot(width_slab, head, preferred_element_type=jnp.flo...  41.5 us
    all_to_all x1, blocking collectives, body(): lax.all_to_all(whole_width, 'ctx', split_axis=1, concat_axis=0, tiled=True)  26.1 us
    pmax x1, blocking collectives, body(): row_max = lax.pmax(local_max, 'vocab')  21.4 us
    all_gather x1, waiting for transfers between devices, body(): lax.all_gather(dlogits, 'ctx', axis=0, tiled=True)  20.4 us
    psum x1, blocking collectives, body(): sum_exp, target_logit = lax.psum((local_sum, local_target), 'vocab')  17.1 us
  transfers between devices with their start and end apart: 4, of which 4 were waited for; matrix products, arithmetic and copies ran while one was open for 0% of the time, Pallas kernels for 0%

commit v1 on v0

--- a/solution.py
+++ b/solution.py
@@ -40,7 +40,10 @@
         (((1,), (1,)), ((), ())),
         preferred_element_type=jnp.float32,
     )
-    returned = lax.all_to_all(grad_slab, "ctx", split_axis=0, concat_axis=1, tiled=True)
+    returned = jnp.concatenate(
+        lax.all_to_all(jnp.stack(jnp.split(grad_slab, lax.axis_size("ctx"), axis=0)), "ctx", 0, 0),
+        axis=1,
+    )
     grad_width = lax.psum_scatter(returned, "vocab", scatter_dimension=1, tiled=True)
     grad_out = grad_width.astype(jnp.bfloat16).reshape(group_rows, depth_count, grad_width.shape[1])
     return (token_loss, grad_out)

time: 361 us -> 358 us (level)
    reshape x0 -> x1, local copies, waits for them, and re-layouts: none -> 5.14 us  [body(): jnp.concatenate(lax.all_to_all(jnp.stack(jnp.split(grad_slab, lax.axis_si...]
    all_to_all x1 -> x0, local copies, waits for them, and re-layouts: 5.12 us -> none  [body(): lax.all_to_all(grad_slab, 'ctx', split_axis=0, concat_axis=1, tiled=True)]
where the time goes in v1:
time: 358 us; the launch traced here: 357 us
  waiting for transfers between devices  194 us (54%)
  blocking collectives  110 us (31%)
  matrix products  16.3 us (5%)
  local copies, waits for them, and re-layouts  16 us (4%)
  between operations  13.9 us (4%)
  other arithmetic  6.79 us (2%)
    reduce_scatter x1, waiting for transfers between devices, body(): lax.psum_scatter(returned, 'vocab', scatter_dimension=1, tiled=True)  80.7 us
    all_gather x1, waiting for transfers between devices, body(): whole_width = lax.all_gather(flat_hidden, 'vocab', axis=1, tiled=True)  51.1 us
    all_to_all x1, blocking collectives, body(): lax.all_to_all(jnp.stack(jnp.split(grad_slab, lax.axis_size('ctx'), axis=...  45.9 us
    reduce_scatter x1, waiting for transfers between devices, body(): lax.psum_scatter(jnp.dot(width_slab, head, preferred_element_type=jnp.flo...  41.5 us
    all_to_all x1, blocking collectives, body(): lax.all_to_all(whole_width, 'ctx', split_axis=1, concat_axis=0, tiled=True)  26.1 us
    pmax x1, blocking collectives, body(): row_max = lax.pmax(local_max, 'vocab')  21.4 us
    all_gather x1, waiting for transfers between devices, body(): lax.all_gather(dlogits, 'ctx', axis=0, tiled=True)  20.4 us
    psum x1, blocking collectives, body(): sum_exp, target_logit = lax.psum((local_sum, local_target), 'vocab')  17.1 us
  transfers between devices with their start and end apart: 4, of which 4 were waited for; matrix products, arithmetic and copies ran while one was open for 0% of the time, Pallas kernels for 0%

profile of v1, /device:TPU:0, one launch (start us, length us, event | category | flops | bytes accessed | tf_op | source)
XLA Modules:
  0.0 357.3 jit_solution(14834097262518159521)
XLA Ops:
  7.2 1.7 reshape.26
  9.0 51.1 %all-gather.3.cloned.1.call-done = bf16[128,7168]{1,0:T(8,128)(2,1)} async-done(((bf16[128,896]{1,0:T(8,128)(2,1)}), bf16[128,7168]{1,0:T(8,128)(2,1)}) %all-gather.3.cloned.1.call-update) | async-done | bytes 1835024 | tf_op jit(solution)/shard_map/all_gather | solution.py:16
  60.1 3.3 copy.21
  63.4 26.1 %all_to_all.24 = bf16[128,4,1792]{0,2,1:T(8,128)(2,1)} all-to-all(bf16[128,4,1792]{0,2,1:T(8,128)(2,1)S(1)} %bitcast.19), channel_id=1, replica_groups=mesh['ctx'=4,'vocab'=8] {'ctx'}, dimensions={1} | all-to-all | bytes 3670016 | tf_op jit(solution)/shard_map/all_to_all | solution.py:17
  89.4 2.8 copy.22
  92.2 8.6 %fusion.5 = f32[512,2048]{1,0:T(8,128)} fusion(bf16[512,1792]{1,0:T(8,128)(2,1)S(1)} %bitcast.21, bf16[1792,2048]{1,0:T(8,128)(2,1)} %param.5), kind=kOutput, calls=%fused_computation.15 | convolution fusion | flops 3758096384 | bytes 13369344 | tf_op jit(solution)/shard_map/dot_general | solution.py:19
  100.9 0.6 copy-done
  101.9 41.5 %reduce-scatter.3.cloned.1.call-done = f32[128,2048]{1,0:T(8,128)} async-done(((f32[512,2048]{1,0:T(8,128)}), f32[128,2048]{1,0:T(8,128)}) %reduce-scatter.3.cloned.1.call-update) | async-done | bytes 1048592 | tf_op jit(solution)/shard_map/reduce_scatter | solution.py:18
  143.5 1.4 reduce_max.9
  144.8 21.4 %pmax.7 = f32[128]{0:T(128)S(1)} all-reduce(f32[128]{0:T(128)S(1)} %reduce_max.9), channel_id=1, replica_groups=mesh['ctx'=4,'vocab'=8] {'vocab'}, use_global_device_ids=true, to_apply=%region_2.3 | all-reduce | flops 128 | bytes 1024 | tf_op jit(solution)/shard_map/pmax | solution.py:28
  166.2 1.6 fusion.4
  167.8 17.1 %all-reduce = (f32[128]{0:T(128)S(1)}, f32[128]{0:T(128)S(1)}) all-reduce(f32[128]{0:T(128)S(1)} %get-tuple-element.11, f32[128]{0:T(128)S(1)} %get-tuple-element.10), channel_id=1, replica_groups=mesh['ctx'=4,'vocab'=8] {'vocab'}, use_global_device_ids=true, to_apply=%region_6.7 | all-reduce | flops 256 | bytes 2048 | tf_op jit(solution)/shard_map/psum | solution.py:30
  184.9 2.4 fusion.3
  187.4 20.4 %all-gather.5.cloned.1.call-done = bf16[512,2048]{1,0:T(8,128)(2,1)} async-done(((bf16[128,2048]{1,0:T(8,128)(2,1)}), bf16[512,2048]{1,0:T(8,128)(2,1)}) %all-gather.5.cloned.1.call-update) | async-done | bytes 2097168 | tf_op jit(solution)/shard_map/all_gather | solution.py:38
  207.9 7.7 %fusion.6 = f32[512,1792]{1,0:T(8,128)S(1)} fusion(bf16[512,2048]{1,0:T(8,128)(2,1)} %all-gather.5.cloned.1.call-done, bf16[1792,2048]{1,0:T(8,128)(2,1)} %param.5), kind=kOutput, calls=%fused_computation.16 | convolution fusion | flops 3758096384 | bytes 13107200 | tf_op jit(solution)/shard_map/dot_general | solution.py:37
  215.6 0.3 slice_bitcast_fusion.3
  215.9 0.4 pad_maximum_fusion
  216.2 45.9 %all_to_all.25 = f32[4,128,1792]{2,1,0:T(8,128)} all-to-all(f32[4,128,1792]{2,1,0:T(8,128)S(1)} %pad_maximum_fusion), channel_id=1, replica_groups=mesh['ctx'=4,'vocab'=8] {'ctx'}, dimensions={0} | all-to-all | bytes 7340032 | tf_op jit(solution)/shard_map/all_to_all | solution.py:44
  262.1 5.1 %copy.25 = f32[128,4,1792]{0,2,1:T(8,128)} copy(f32[128,4,1792]{2,0,1:T(8,128)} %bitcast.18) | data formatting | bytes 7340032 | tf_op jit(solution)/shard_map/reshape | solution.py:43
  267.4 0.6 copy.27
  268.1 80.7 %reduce-scatter.5.cloned.1.call-done = f32[128,896]{0,1:T(8,128)} async-done(((f32[128,7168]{0,1:T(8,128)}), f32[128,896]{0,1:T(8,128)}) %reduce-scatter.5.cloned.1.call-update) | async-done | bytes 458768 | tf_op jit(solution)/shard_map/reduce_scatter | solution.py:47
  348.8 1.0 convert_element_type.11
  349.8 0.2 copy.26
  350.0 0.8 reshape.30
  (18 shorter events, 0.8 us)
Async XLA Ops:
  7.2 52.9 %all-gather.3.cloned.1.call-start = ((), (), s32[]{:S(2)}) async-start(), calls=%async_computation.4 | async-start | bytes 2064384 | tf_op jit(solution)/shard_map/all_gather | solution.py:16
  8.9 134.5 %reduce-scatter.3.cloned.1.call-start = ((), (), s32[]{:S(2)}) async-start(), calls=%async_computation.5 | async-start | bytes 5242880 | tf_op jit(solution)/shard_map/reduce_scatter | solution.py:18
  100.8 0.7 copy-start
  100.8 0.9 copy-start.1
  100.8 107.1 %all-gather.5.cloned.1.call-start = ((), (), s32[]{:S(2)}) async-start(), calls=%async_computation.6 | async-start | bytes 2621440 | tf_op jit(solution)/shard_map/all_gather | solution.py:38
  187.4 161.4 %reduce-scatter.5.cloned.1.call-start = ((), (), s32[]{:S(2)}) async-start(), calls=%async_computation.7 | async-start | bytes 4128768 | tf_op jit(solution)/shard_map/reduce_scatter | solution.py:47
Sparse Core Ops, SparseCore 0:
  10.8 49.2 all-gather.2
  100.9 42.4 reduce-scatter.2
  187.5 20.3 all-gather.4
  267.4 81.2 reduce-scatter.4
